TPU v7x, 64 devices: a 2x2x8 block of a 4x4x8 slice. The times are simulated.
64 devices in a mesh: dp: 8 (over x, y, core), tp: 8 (over z).
Axes of the slice: x: 2, y: 2, z: 8, core: 2. Of those that a mesh axis runs over, the one named last changes fastest.
The devices are a block of a 4x4x8 slice.
Arguments:
- x: bfloat16 [16384, 2560], P('dp'), parts along dimension 0
- dy: bfloat16 [16384, 2560], P('dp'), parts along dimension 0
- gate: bfloat16 [16384, 10240], P('dp', 'tp'), parts along dimension 0
- up: bfloat16 [16384, 10240], P('dp', 'tp'), parts along dimension 0
- w_gate: bfloat16 [2560, 10240], P(None, 'tp')
- w_up: bfloat16 [2560, 10240], P(None, 'tp')
- w_down: bfloat16 [10240, 2560], P('tp')
Outputs:
- output 1: bfloat16 [16384, 2560], P('dp'), parts along dimension 0
- output 2: bfloat16 [20480, 10240], P('dp', 'tp'), parts along dimension 0
- output 3: bfloat16 [20480, 10240], P('dp', 'tp'), parts along dimension 0
- output 4: bfloat16 [81920, 2560], P(('dp', 'tp')), parts along dimension 0
There are 8 independent parts. A program takes and returns all parts, laid end to end along the dimension named above; an argument that names none is the same for every part.
All inputs are finite; a program needn't handle non-finite values.
Results may differ from a plain program's by a relative error of at most 0.012.
Values are sent between devices in bfloat16 or wider.
A program may use at most 768 MiB of HBM per device.

v0:
```python
import functools

import jax
import jax.numpy as jnp
from jax import lax
from jax.experimental import pallas as pl
from jax.experimental.pallas import tpu as pltpu
from jax.sharding import PartitionSpec as P

BF = jnp.bfloat16
F32 = jnp.float32
W = 256
MESH = pl.DeviceIdType.MESH
ROOT = 0.7978845608028654
CUBE = 0.044715


def nt(a, b):
    return lax.dot_general(a, b, (((1,), (1,)), ((), ())), preferred_element_type=F32)


def tn(a, b):
    return lax.dot_general(a, b, (((0,), (0,)), ((), ())), preferred_element_type=F32)


def kernel(n, x, dy, gate, up, wg, wu, wd, dx, dwg, dwu, dwd,
           dy_v, dgu, hid, wd_v, wgu, buf, xt, ost,
           rs_send, rs_recv, ag_send, ag_recv, in_sem, wd_sem, w_sem, own_sem, x_sem, o_sem):
    T, D = x.shape
    F = gate.shape[1]
    R = T // n
    H = D // 2
    C = H // W
    FT = F // W
    me = lax.axis_index("tp")
    right, left = lax.rem(me + 1, n), lax.rem(me + n - 1, n)
    to = (right, left)

    def mod(b):
        return lax.rem(b + 2 * n, n)

    def ds(i, size):
        return pl.ds(pl.multiple_of(i * size, size), size)

    def load_block(b):
        rows = ds(b, R)
        return (pltpu.make_async_copy(dy.at[rows, :], dy_v.at[rows, :], in_sem.at[0, b]),
                pltpu.make_async_copy(gate.at[rows, :], dgu.at[0, rows, :], in_sem.at[1, b]),
                pltpu.make_async_copy(up.at[rows, :], dgu.at[1, rows, :], in_sem.at[2, b]))

    def load_wd(j):
        return pltpu.make_async_copy(wd.at[ds(j, W), :], wd_v.at[ds(j, W), :], wd_sem.at[j])

    def load_w(t):
        return (pltpu.make_async_copy(wg.at[ds(t, W), :], wgu.at[0, ds(t, W), :], w_sem.at[0, t]),
                pltpu.make_async_copy(wu.at[ds(t, W), :], wgu.at[1, ds(t, W), :], w_sem.at[1, t]))

    def load_x(i, k):
        return pltpu.make_async_copy(x.at[:, ds(i, W)], xt.at[k], x_sem.at[k])

    def rs(d, s, j):
        return pltpu.make_async_remote_copy(
            src_ref=buf.at[d, s, j], dst_ref=buf.at[d, s + 1, j],
            send_sem=rs_send.at[d, s, j], recv_sem=rs_recv.at[d, s, j],
            device_id={"tp": to[d]}, device_id_type=MESH)

    def rs_block(d, s):
        return mod(me - 1 - s) if d == 0 else mod(me - 1 + s)

    def piece(d, b, j):
        return dx.at[ds(b, R), ds(d * C + j, W)]

    def ag_first(d, j):
        b = rs_block(d, n - 1)
        return pltpu.make_async_remote_copy(
            src_ref=buf.at[d, n - 1, j], dst_ref=piece(d, b, j),
            send_sem=ag_send.at[d, 0, j], recv_sem=ag_recv.at[d, 0, j],
            device_id={"tp": to[d]}, device_id_type=MESH)

    def ag_own(d, j):
        return pltpu.make_async_copy(buf.at[d, n - 1, j], piece(d, rs_block(d, n - 1), j), own_sem.at[d, j])

    def ag(d, a, j, b):
        return pltpu.make_async_remote_copy(
            src_ref=piece(d, b, j), dst_ref=piece(d, b, j),
            send_sem=ag_send.at[d, a, j], recv_sem=ag_recv.at[d, a, j],
            device_id={"tp": to[d]}, device_id_type=MESH)

    def ag_in(d, a):
        return mod(me - 1 - a) if d == 0 else mod(me - 1 + a)

    def wait_block(b):
        for c in load_block(b):
            c.wait()

    def dh(b, j):
        rows, cols = ds(b, R), ds(j, W)
        d = nt(dy_v[rows, :], wd_v[cols, :])
        g = dgu[0, rows, cols].astype(F32)
        u = dgu[1, rows, cols].astype(F32)
        g2 = g * g
        t = jnp.tanh(ROOT * (g + CUBE * (g2 * g)))
        cdf = 0.5 * (1.0 + t)
        act = g * cdf
        slope = cdf + g * (0.5 * (1.0 - t * t)) * (ROOT * (1.0 + (3.0 * CUBE) * g2))
        hid[rows, cols] = (act * u).astype(BF)
        dgu[0, rows, cols] = (d * u * slope).astype(BF)
        dgu[1, rows, cols] = (d * act).astype(BF)

    def term(d, s, j):
        rows, tile = ds(rs_block(d, s), R), ds(d * C + j, W)
        return nt(dgu[0, rows, :], wgu[0, tile, :]) + nt(dgu[1, rows, :], wgu[1, tile, :])

    def rs_slot(s, j, first=False, last=False, blocks=()):
        if first:
            for d in (0, 1):
                for c in load_w(d * C + j):
                    c.wait()
        else:
            for d in (0, 1):
                rs(d, s - 1, j).wait_recv()
        if blocks:
            @pl.when(j == 0)
            def _():
                for b in blocks:
                    wait_block(b)
        sums = [term(d, s, j) for d in (0, 1)]
        if not first:
            sums = [buf[d, s, j].astype(F32) + sums[d] for d in (0, 1)]
        for d in (0, 1):
            buf[d, s, j] = sums[d].astype(BF)
        for d in (0, 1):
            if last:
                ag_first(d, j).start()
                ag_own(d, j).start()
            else:
                rs(d, s, j).start()
        for b in blocks:
            dh(b, j)

    order = [mod(me - 1), mod(me - 2), me, mod(me - 3), mod(me + 1), mod(me - 4), mod(me + 2), mod(me + 3)]
    for c in load_block(order[0]):
        c.start()
    for j in range(FT):
        load_wd(j).start()
    for j in range(C):
        for d in (0, 1):
            for c in load_w(d * C + j):
                c.start()
    for b in order[1:]:
        for c in load_block(b):
            c.start()
    for k in (0, 1):
        load_x(k, k).start()

    barrier = pltpu.get_barrier_semaphore()
    for p in (left, right):
        pl.semaphore_signal(barrier, inc=1, device_id={"tp": p}, device_id_type=MESH)
    pl.semaphore_wait(barrier, 2)

    wait_block(order[0])

    @pl.loop(0, FT)
    def _(j):
        load_wd(j).wait()
        dh(order[0], j)

    @pl.loop(0, C)
    def _(j):
        rs_slot(0, j, first=True, blocks=(mod(me - 2), me))

    @pl.loop(0, 2 * C)
    def _(q):
        s, j = q // C + 1, lax.rem(q, C)
        rs_slot(s, j, blocks=(mod(me - 2 - s), mod(me + s)))

    @pl.loop(0, C)
    def _(j):
        rs_slot(3, j, blocks=(mod(me + 3),))

    @pl.loop(0, (n - 5) * C)
    def _(q):
        rs_slot(q // C + 4, lax.rem(q, C))

    @pl.loop(0, C)
    def _(j):
        rs_slot(n - 1, j, last=True)

    @pl.loop(0, (n - 1) * C)
    def _(q):
        for d in (0, 1):
            rs(d, q // C, lax.rem(q, C)).wait_send()

    def forward(q):
        a, j = q // C, lax.rem(q, C)
        for d in (0, 1):
            b = ag_in(d, a)
            ag(d, a, j, b).wait_recv()

            @pl.when(a < n - 2)
            def _():
                ag(d, a + 1, j, b).start()

    def put(k, dst):
        return pltpu.make_async_copy(ost.at[k], dst, o_sem.at[k])

    @pl.loop(0, D // W)
    def _(i):
        k = lax.rem(i, 2)
        load_x(i, k).wait()
        for h, out in ((0, dwg), (1, dwu)):
            @pl.when(i > 0)
            def _():
                put(h, out.at[ds(i - 1, W), :]).wait()
            ost[h] = tn(xt[k], dgu[h]).astype(BF)
            put(h, out.at[ds(i, W), :]).start()
            forward(2 * i + h)

        @pl.when(i + 2 < D // W)
        def _():
            load_x(i + 2, k).start()

    @pl.loop(0, FT)
    def _(i):
        for h in (0, 1):
            put(h, dwd.at[ds(0, W), ds(h, H)]).wait()
            ost[h] = tn(hid[:, ds(i, W)], dy_v[:, h * H:(h + 1) * H]).astype(BF)
            put(h, dwd.at[ds(i, W), ds(h, H)]).start()
            forward(2 * (D // W) + 2 * i + h)

    @pl.loop(2 * (D // W) + 2 * FT, (n - 1) * C)
    def _(q):
        forward(q)

    for h in (0, 1):
        put(h, dwd.at[ds(0, W), ds(h, H)]).wait()

    @pl.loop(0, C)
    def _(j):
        for d in (0, 1):
            ag_own(d, j).wait()
            ag_first(d, j).wait_send()

    @pl.loop(C, (n - 1) * C)
    def _(q):
        for d in (0, 1):
            ag(d, q // C, lax.rem(q, C), me).wait_send()


def solution(mesh):
    n = mesh.shape["tp"]

    def step(x, dy, gate, up, w_gate, w_up, w_down):
        T, D = x.shape
        F = gate.shape[1]
        R, C, FT = T // n, D // 2 // W, F // W
        assert C == FT and n == 8
        dma = pltpu.SemaphoreType.DMA
        any_ = pl.BlockSpec(memory_space=pl.ANY)
        return pl.pallas_call(
            functools.partial(kernel, n),
            out_shape=[jax.ShapeDtypeStruct(s, BF) for s in ((T, D), (D, F), (D, F), (F, D))],
            in_specs=[any_] * 7,
            out_specs=[any_] * 4,
            scratch_shapes=[
                pltpu.VMEM((T, D), BF),
                pltpu.VMEM((2, T, F), BF),
                pltpu.VMEM((T, F), BF),
                pltpu.VMEM((F, D), BF),
                pltpu.VMEM((2, D, F), BF),
                pltpu.VMEM((2, n, C, R, W), BF),
                pltpu.VMEM((2, T, W), BF),
                pltpu.VMEM((2, W, F), BF),
                dma((2, n - 1, C)), dma((2, n - 1, C)), dma((2, n - 1, C)), dma((2, n - 1, C)),
                dma((3, n)), dma((FT,)), dma((2, 2 * C)), dma((2, C)), dma((2,)), dma((2,)),
            ],
            compiler_params=pltpu.CompilerParams(
                collective_id=0, has_side_effects=True, vmem_limit_bytes=67043328),
            name="mlp_bwd",
        )(x, dy, gate, up, w_gate, w_up, w_down)

    tokens, columns, rows = P("dp", None), P(None, "tp"), P("tp", None)
    return jax.shard_map(
        step,
        mesh=mesh,
        in_specs=(tokens, tokens, P("dp", "tp"), P("dp", "tp"), columns, columns, rows),
        out_specs=(tokens, P("dp", "tp"), P("dp", "tp"), P(("dp", "tp"), None)),
        check_vma=False,
    )
```

profile of v0, /device:TPU:22, one launch (start us, length us, event | category | flops | bytes accessed | tf_op | source)
XLA Modules:
  0.0 246.1 jit_solution(17786731235052487256)
XLA Ops:
  0.6 222.5 %mlp_bwd.1 = (bf16[2048,2560]{1,0:T(8,128)(2,1)}, bf16[2560,1280]{1,0:T(8,128)(2,1)}, bf16[2560,1280]{1,0:T(8,128)(2,1)}, bf16[1280,2560]{1,0:T(8,128)(2,1)}) custom-call(bf16[2048,2560]{1,0:T(8,128)(2,1)} %x.1, bf16[2048,2560]{1,0:T(8,128)(2,1)} %dy.1, bf16[2048,1280]{1,0:T(8,128)(2,1)} %gate.1, bf16[2048,1280]{1,0:T(8,128)(2,1)} %up.1, ...), custom_call_target="tpu_custom_call" | custom-call | tf_op jit(solution)/shard_map/mlp_bwd/pallas_call | solution.py:260
  223.1 8.7 %copy.15 = bf16[2048,2560]{1,0:T(8,128)(2,1)} copy(bf16[2048,2560]{1,0:T(8,128)(2,1)} %get-tuple-element.8) | data formatting | bytes 20971520
  231.8 0.0 copy-start
  231.8 0.0 slice-start
  231.8 6.8 %copy.16 = bf16[2560,1280]{1,0:T(8,128)(2,1)} copy(bf16[2560,1280]{1,0:T(8,128)(2,1)} %get-tuple-element.9) | data formatting | bytes 13107200
  238.6 0.0 copy-done
  238.6 0.0 slice-start.1
  238.6 3.3 %copy.17 = bf16[2560,1280]{1,0:T(8,128)(2,1)} copy(bf16[2560,1280]{1,0:T(8,128)(2,1)S(1)} %copy-done) | data formatting | bytes 13107200
  241.9 0.0 slice-done
  241.9 1.4 slice-done.1
  243.3 2.8 %copy.18 = bf16[1280,2560]{1,0:T(8,128)(2,1)} copy(bf16[1280,2560]{1,0:T(8,128)(2,1)S(1)} %bitcast.1) | data formatting | bytes 13107200
  (1 shorter events, 0.0 us)
Async XLA Ops:
  231.8 6.8 %copy-start = (bf16[2560,1280]{1,0:T(8,128)(2,1)S(1)}, bf16[2560,1280]{1,0:T(8,128)(2,1)}, u32[]{:S(2)}) copy-start(bf16[2560,1280]{1,0:T(8,128)(2,1)} %get-tuple-element.10) | copy-start | bytes 19660804
  231.8 10.1 %slice-start = ((s8[6553600]{0:T(1024)(128)(4,1)}), s8[4194304]{0:T(1024)(128)(4,1)S(1)}, s32[]{:S(2)}) async-start(s8[6553600]{0:T(1024)(128)(4,1)} %bitcast), calls=%async_computation | async-start | bytes 8388608
  238.6 4.7 %slice-start.1 = ((s8[6553600]{0:T(1024)(128)(4,1)}), s8[2359296]{0:T(1024)(128)(4,1)S(1)}, s32[]{:S(2)}) async-start(s8[6553600]{0:T(1024)(128)(4,1)} %bitcast), calls=%async_computation.1 | async-start | bytes 4718592
where the time goes:
time: 247 us; the launch traced here: 246 us
  Pallas kernels  222 us (90%)
  local copies, waits for them, and re-layouts  23 us (9%)
    pallas_call x1, Pallas kernels, step(): pl.pallas_call(functools.partial(kernel, n), out_shape=[jax.ShapeDtypeStr...  222 us
    unnamed x10, local copies, waits for them, and re-layouts  23 us

commit v1 on v0

--- a/solution.py
+++ b/solution.py
@@ -23,9 +23,9 @@
     return lax.dot_general(a, b, (((0,), (0,)), ((), ())), preferred_element_type=F32)
 
 
-def kernel(n, x, dy, gate, up, wg, wu, wd, dx, dwg, dwu, dwd,
-           dy_v, dgu, hid, wd_v, wgu, buf, xt, ost,
-           rs_send, rs_recv, ag_send, ag_recv, in_sem, wd_sem, w_sem, own_sem, x_sem, o_sem):
+def kernel(n, x, dy, gate, up, wg, wu, wd, dx, end_r, end_l, dwg, dwu, dwd,
+           dy_v, dgu, hid, buf, xt,
+           rs_send, rs_recv, ag_send, ag_recv, in_sem, wd_sem, w_sem, own_sem, x_sem):
     T, D = x.shape
     F = gate.shape[1]
     R = T // n
@@ -49,11 +49,11 @@
                 pltpu.make_async_copy(up.at[rows, :], dgu.at[1, rows, :], in_sem.at[2, b]))
 
     def load_wd(j):
-        return pltpu.make_async_copy(wd.at[ds(j, W), :], wd_v.at[ds(j, W), :], wd_sem.at[j])
+        return pltpu.make_async_copy(wd.at[ds(j, W), :], dwd.at[ds(j, W), :], wd_sem.at[j])
 
     def load_w(t):
-        return (pltpu.make_async_copy(wg.at[ds(t, W), :], wgu.at[0, ds(t, W), :], w_sem.at[0, t]),
-                pltpu.make_async_copy(wu.at[ds(t, W), :], wgu.at[1, ds(t, W), :], w_sem.at[1, t]))
+        return (pltpu.make_async_copy(wg.at[ds(t, W), :], dwg.at[ds(t, W), :], w_sem.at[0, t]),
+                pltpu.make_async_copy(wu.at[ds(t, W), :], dwu.at[ds(t, W), :], w_sem.at[1, t]))
 
     def load_x(i, k):
         return pltpu.make_async_copy(x.at[:, ds(i, W)], xt.at[k], x_sem.at[k])
@@ -86,6 +86,12 @@
             send_sem=ag_send.at[d, a, j], recv_sem=ag_recv.at[d, a, j],
             device_id={"tp": to[d]}, device_id_type=MESH)
 
+    def ag_end(d, j, b):
+        return pltpu.make_async_remote_copy(
+            src_ref=piece(d, b, j), dst_ref=(end_r, end_l)[d].at[:, ds(j, W)],
+            send_sem=ag_send.at[d, n - 3, j], recv_sem=ag_recv.at[d, n - 3, j],
+            device_id={"tp": to[d]}, device_id_type=MESH)
+
     def ag_in(d, a):
         return mod(me - 1 - a) if d == 0 else mod(me - 1 + a)
 
@@ -95,7 +101,7 @@
 
     def dh(b, j):
         rows, cols = ds(b, R), ds(j, W)
-        d = nt(dy_v[rows, :], wd_v[cols, :])
+        d = nt(dy_v[rows, :], dwd[cols, :])
         g = dgu[0, rows, cols].astype(F32)
         u = dgu[1, rows, cols].astype(F32)
         g2 = g * g
@@ -109,7 +115,7 @@
 
     def term(d, s, j):
         rows, tile = ds(rs_block(d, s), R), ds(d * C + j, W)
-        return nt(dgu[0, rows, :], wgu[0, tile, :]) + nt(dgu[1, rows, :], wgu[1, tile, :])
+        return nt(dgu[0, rows, :], dwg[tile, :]) + nt(dgu[1, rows, :], dwu[tile, :])
 
     def rs_slot(s, j, first=False, last=False, blocks=()):
         if first:
@@ -139,19 +145,18 @@
             dh(b, j)
 
     order = [mod(me - 1), mod(me - 2), me, mod(me - 3), mod(me + 1), mod(me - 4), mod(me + 2), mod(me + 3)]
-    for c in load_block(order[0]):
-        c.start()
-    for j in range(FT):
-        load_wd(j).start()
-    for j in range(C):
-        for d in (0, 1):
-            for c in load_w(d * C + j):
-                c.start()
-    for b in order[1:]:
-        for c in load_block(b):
+
+    def start(copies):
+        for c in copies:
             c.start()
-    for k in (0, 1):
-        load_x(k, k).start()
+
+    def start_w(j):
+        for d in (0, 1):
+            start(load_w(d * C + j))
+
+    start(load_block(order[0]))
+    start([load_wd(j) for j in range(FT)])
+    start_w(0)
 
     barrier = pltpu.get_barrier_semaphore()
     for p in (left, right):
@@ -163,10 +168,22 @@
     @pl.loop(0, FT)
     def _(j):
         load_wd(j).wait()
+
+        @pl.when(j + 1 < C)
+        def _():
+            start_w(j + 1)
+        for k in (0, 1):
+            @pl.when(j == k)
+            def _():
+                start(load_block(order[k + 1]))
         dh(order[0], j)
 
     @pl.loop(0, C)
     def _(j):
+        for k in range(5):
+            @pl.when(j == k)
+            def _():
+                start(load_block(order[k + 3]))
         rs_slot(0, j, first=True, blocks=(mod(me - 2), me))
 
     @pl.loop(0, 2 * C)
@@ -182,6 +199,9 @@
     def _(q):
         rs_slot(q // C + 4, lax.rem(q, C))
 
+    for k in (0, 1):
+        load_x(k, k).start()
+
     @pl.loop(0, C)
     def _(j):
         rs_slot(n - 1, j, last=True)
@@ -195,25 +215,29 @@
         a, j = q // C, lax.rem(q, C)
         for d in (0, 1):
             b = ag_in(d, a)
-            ag(d, a, j, b).wait_recv()
-
-            @pl.when(a < n - 2)
+
+            @pl.when(a < n - 3)
+            def _():
+                ag(d, a, j, b).wait_recv()
+
+            @pl.when(a < n - 4)
             def _():
                 ag(d, a + 1, j, b).start()
 
-    def put(k, dst):
-        return pltpu.make_async_copy(ost.at[k], dst, o_sem.at[k])
+            @pl.when(a == n - 4)
+            def _():
+                ag_end(d, j, b).start()
+
+            @pl.when(a == n - 3)
+            def _():
+                ag_end(d, j, b).wait_recv()
 
     @pl.loop(0, D // W)
     def _(i):
         k = lax.rem(i, 2)
         load_x(i, k).wait()
         for h, out in ((0, dwg), (1, dwu)):
-            @pl.when(i > 0)
-            def _():
-                put(h, out.at[ds(i - 1, W), :]).wait()
-            ost[h] = tn(xt[k], dgu[h]).astype(BF)
-            put(h, out.at[ds(i, W), :]).start()
+            out[ds(i, W), :] = tn(xt[k], dgu[h]).astype(BF)
             forward(2 * i + h)
 
         @pl.when(i + 2 < D // W)
@@ -223,28 +247,64 @@
     @pl.loop(0, FT)
     def _(i):
         for h in (0, 1):
-            put(h, dwd.at[ds(0, W), ds(h, H)]).wait()
-            ost[h] = tn(hid[:, ds(i, W)], dy_v[:, h * H:(h + 1) * H]).astype(BF)
-            put(h, dwd.at[ds(i, W), ds(h, H)]).start()
+            dwd[ds(i, W), h * H:(h + 1) * H] = tn(hid[:, ds(i, W)], dy_v[:, h * H:(h + 1) * H]).astype(BF)
             forward(2 * (D // W) + 2 * i + h)
-
-    @pl.loop(2 * (D // W) + 2 * FT, (n - 1) * C)
-    def _(q):
-        forward(q)
-
-    for h in (0, 1):
-        put(h, dwd.at[ds(0, W), ds(h, H)]).wait()
 
     @pl.loop(0, C)
     def _(j):
         for d in (0, 1):
             ag_own(d, j).wait()
             ag_first(d, j).wait_send()
-
-    @pl.loop(C, (n - 1) * C)
+            ag_end(d, j, me).wait_send()
+
+    @pl.loop(C, (n - 3) * C)
     def _(q):
         for d in (0, 1):
             ag(d, q // C, lax.rem(q, C), me).wait_send()
+
+
+def half(ref, b, R, d):
+    H = ref.shape[1] // 2
+    return ref.at[pl.ds(pl.multiple_of(b * R, R), R), d * H:(d + 1) * H]
+
+
+def copy_kernel(n, dx, end_r, end_l, dwg, dwu, dwd, dx_o, dwg_o, dwu_o, dwd_o, stage, in_sem, out_sem, w_sem):
+    R = dx.shape[0] // n
+    me = lax.axis_index("tp")
+    parts = []
+    for d, end in ((0, end_r), (1, end_l)):
+        for a in range(-1, n - 2):
+            b = lax.rem((me - 1 - a if d == 0 else me - 1 + a) + 2 * n, n)
+            if d == 1 and a == -1:
+                b = lax.rem(me - 2 + n, n)
+            src = end if a == n - 3 else half(dx, b, R, d)
+            i = len(parts)
+            parts.append((pltpu.make_async_copy(src, stage.at[i], in_sem.at[i]),
+                          pltpu.make_async_copy(stage.at[i], half(dx_o, b, R, d), out_sem.at[i])))
+    whole = [pltpu.make_async_copy(v, o, w_sem.at[i])
+             for i, (v, o) in enumerate(((dwg, dwg_o), (dwu, dwu_o), (dwd, dwd_o)))]
+    for load, _ in parts:
+        load.start()
+    for c in whole:
+        c.start()
+    for load, store in parts:
+        load.wait()
+        store.start()
+    for c in whole:
+        c.wait()
+    for _, store in parts:
+        store.wait()
+
+
+def end_kernel(n, dx, got_r, got_l, dx_o, sem):
+    R = dx.shape[0] // n
+    me = lax.axis_index("tp")
+    copies = [pltpu.make_async_copy(got_r, half(dx_o, lax.rem(me + 1, n), R, 0), sem.at[0]),
+              pltpu.make_async_copy(got_l, half(dx_o, lax.rem(me + n - 3, n), R, 1), sem.at[1])]
+    for c in copies:
+        c.start()
+    for c in copies:
+        c.wait()
 
 
 def solution(mesh):
@@ -257,27 +317,54 @@
         assert C == FT and n == 8
         dma = pltpu.SemaphoreType.DMA
         any_ = pl.BlockSpec(memory_space=pl.ANY)
-        return pl.pallas_call(
+        vmem = pl.BlockSpec(memory_space=pltpu.VMEM)
+        hbm = pl.BlockSpec(memory_space=pltpu.HBM)
+        shape = lambda *s: jax.ShapeDtypeStruct(s, BF)
+        dws = [shape(D, F), shape(D, F), shape(F, D)]
+        dx, end_r, end_l, *dw = pl.pallas_call(
             functools.partial(kernel, n),
-            out_shape=[jax.ShapeDtypeStruct(s, BF) for s in ((T, D), (D, F), (D, F), (F, D))],
+            out_shape=[shape(T, D), shape(R, D // 2), shape(R, D // 2)] + [pltpu.VMEM(w.shape, BF) for w in dws],
             in_specs=[any_] * 7,
-            out_specs=[any_] * 4,
+            out_specs=[any_] * 3 + [vmem] * 3,
             scratch_shapes=[
                 pltpu.VMEM((T, D), BF),
                 pltpu.VMEM((2, T, F), BF),
                 pltpu.VMEM((T, F), BF),
-                pltpu.VMEM((F, D), BF),
-                pltpu.VMEM((2, D, F), BF),
                 pltpu.VMEM((2, n, C, R, W), BF),
                 pltpu.VMEM((2, T, W), BF),
-                pltpu.VMEM((2, W, F), BF),
-                dma((2, n - 1, C)), dma((2, n - 1, C)), dma((2, n - 1, C)), dma((2, n - 1, C)),
-                dma((3, n)), dma((FT,)), dma((2, 2 * C)), dma((2, C)), dma((2,)), dma((2,)),
+                dma((2, n - 1, C)), dma((2, n - 1, C)), dma((2, n - 2, C)), dma((2, n - 2, C)),
+                dma((3, n)), dma((FT,)), dma((2, 2 * C)), dma((2, C)), dma((2,)),
             ],
             compiler_params=pltpu.CompilerParams(
-                collective_id=0, has_side_effects=True, vmem_limit_bytes=67043328),
+                collective_id=0, has_side_effects=True, vmem_limit_bytes=44 << 20),
             name="mlp_bwd",
         )(x, dy, gate, up, w_gate, w_up, w_down)
+        ahead = [(i, (i + 1) % n) for i in range(n)]
+        back = [(i, (i - 1) % n) for i in range(n)]
+        got_r = lax.ppermute(end_r, "tp", ahead)
+        got_l = lax.ppermute(end_l, "tp", back)
+        m = 2 * (n - 1)
+        dx, *dw = pl.pallas_call(
+            functools.partial(copy_kernel, n),
+            out_shape=[shape(T, D)] + dws,
+            in_specs=[hbm] * 3 + [vmem] * 3,
+            out_specs=[hbm] * 4,
+            scratch_shapes=[pltpu.VMEM((m, R, D // 2), BF), dma((m,)), dma((m,)), dma((3,))],
+            compiler_params=pltpu.CompilerParams(vmem_limit_bytes=10 << 20),
+            cost_estimate=pl.CostEstimate(flops=13_000_000_000, bytes_accessed=41_000_000, transcendentals=0),
+            name="place",
+        )(*(pltpu.with_memory_space_constraint(v, pltpu.HBM) for v in (dx, end_r, end_l)), *dw)
+        dx = pl.pallas_call(
+            functools.partial(end_kernel, n),
+            out_shape=shape(T, D),
+            in_specs=[any_, vmem, vmem],
+            out_specs=any_,
+            scratch_shapes=[dma((2,))],
+            input_output_aliases={0: 0},
+            compiler_params=pltpu.CompilerParams(vmem_limit_bytes=1 << 20),
+            name="place_end",
+        )(dx, got_r, got_l)
+        return dx, *dw
 
     tokens, columns, rows = P("dp", None), P(None, "tp"), P("tp", None)
     return jax.shard_map(

time: 247 us -> 221 us (0.89)
  local copies, waits for them, and re-layouts: 23 us -> 0 us
  Pallas kernels: 222 us -> 215 us
  starting transfers between devices: 0 us -> 3.32 us
    unnamed x10 -> x0, local copies, waits for them, and re-layouts: 23 us -> none
    pallas_call x1 -> x3, Pallas kernels: 222 us -> 215 us  [the longest x1 202 us: step(): pl.pallas_call(functools.partial(kernel, n), out_shape=[shape(T, D), shap...]
    ppermute x0 -> x2, starting transfers between devices: none -> 3.32 us  [the longest x1 3.21 us: step(): got_l = lax.ppermute(end_l, 'tp', back)]
  transfers between devices with their start and end apart: 0 -> 2, of which waited for: 0 -> 1; matrix products, arithmetic and copies ran while one was open for 0% -> 0% of each run, Pallas kernels for 0% -> 6%
where the time goes in v1:
time: 221 us
  Pallas kernels  215 us (97%)
  starting transfers between devices  3.32 us (2%)
    pallas_call x1, Pallas kernels, step(): pl.pallas_call(functools.partial(kernel, n), out_shape=[shape(T, D), shap...  202 us
    pallas_call x1, Pallas kernels, step(): pl.pallas_call(functools.partial(copy_kernel, n), out_shape=[shape(T, D)]...  12.4 us
  transfers between devices with their start and end apart: 2, of which 1 were waited for; matrix products, arithmetic and copies ran while one was open for 0% of the time, Pallas kernels for 6%

profile of v1, /device:TPU:22, one launch (start us, length us, event | category | flops | bytes accessed | tf_op | source)
XLA Modules:
  0.0 221.3 jit_solution(17442161267195472096)
XLA Ops:
  0.6 202.0 %mlp_bwd.1 = (bf16[2048,2560]{1,0:T(8,128)(2,1)}, bf16[256,1280]{1,0:T(8,128)(2,1)}, bf16[256,1280]{1,0:T(8,128)(2,1)}, bf16[2560,1280]{1,0:T(8,128)(2,1)S(1)}, ...) custom-call(bf16[2048,2560]{1,0:T(8,128)(2,1)} %x.1, bf16[2048,2560]{1,0:T(8,128)(2,1)} %dy.1, ...), custom_call_target="tpu_custom_call" | custom-call | tf_op jit(solution)/shard_map/mlp_bwd/pallas_call | solution.py:324
  202.6 0.1 collective-permute-start
  202.8 3.2 %collective-permute-start.1 = (bf16[256,1280]{1,0:T(8,128)(2,1)}, bf16[256,1280]{1,0:T(8,128)(2,1)S(1)}, u32[]{:S(2)}, u32[]{:S(2)}) collective-permute-start(bf16[256,1280]{1,0:T(8,128)(2,1)} %get-tuple-element.16.end_l), channel_id=1, source_target_pairs={{0,7},{1,0},{2,1},{3,2},{4,3},{5,4},{6,5},{7,6},{8,15},{9,8},{10,9... | collective-permute-start | bytes 1966088 | tf_op jit(solution)/shard_map/ppermute | solution.py:345
  206.0 12.4 %place.1 = (bf16[2048,2560]{1,0:T(8,128)(2,1)}, bf16[2560,1280]{1,0:T(8,128)(2,1)}, bf16[2560,1280]{1,0:T(8,128)(2,1)}, bf16[1280,2560]{1,0:T(8,128)(2,1)}) custom-call(bf16[2048,2560]{1,0:T(8,128)(2,1)} %get-tuple-element.14.dx, bf16[256,1280]{1,0:T(8,128)(2,1)} %get-tuple-element.15.end_r, bf16[256,1280]{1,0:T(8,128)(2,1)} %get-tuple-element.16.end_l, ...), custom_call_target="tpu_custom_call" | custom-call | flops 12999999488 | bytes 41000000 | tf_op jit(solution)/shard_map/place/pallas_call | solution.py:347
  218.4 1.9 collective-permute-done.got_r
  220.3 0.0 collective-permute-done.1.got_l
  220.3 1.1 place_end.1
Async XLA Ops:
  202.6 17.6 %collective-permute-start = (bf16[256,1280]{1,0:T(8,128)(2,1)}, bf16[256,1280]{1,0:T(8,128)(2,1)S(1)}, u32[]{:S(2)}, u32[]{:S(2)}) collective-permute-start(bf16[256,1280]{1,0:T(8,128)(2,1)} %get-tuple-element.15.end_r), channel_id=1, source_target_pairs={{0,1},{1,2},{2,3},{3,4},{4,5},{5,6},{6,7},{7,0},{8,9},{9,10},{10,1... | collective-permute-start | bytes 1966088 | tf_op jit(solution)/shard_map/ppermute | solution.py:344
  202.8 17.5 %collective-permute-start.1 = (bf16[256,1280]{1,0:T(8,128)(2,1)}, bf16[256,1280]{1,0:T(8,128)(2,1)S(1)}, u32[]{:S(2)}, u32[]{:S(2)}) collective-permute-start(bf16[256,1280]{1,0:T(8,128)(2,1)} %get-tuple-element.16.end_l), channel_id=1, source_target_pairs={{0,7},{1,0},{2,1},{3,2},{4,3},{5,4},{6,5},{7,6},{8,15},{9,8},{10,9... | collective-permute-start | bytes 1966088 | tf_op jit(solution)/shard_map/ppermute | solution.py:345

commit v2 on v1

--- a/solution.py
+++ b/solution.py
@@ -25,7 +25,7 @@
 
 def kernel(n, x, dy, gate, up, wg, wu, wd, dx, end_r, end_l, dwg, dwu, dwd,
            dy_v, dgu, hid, buf, xt,
-           rs_send, rs_recv, ag_send, ag_recv, in_sem, wd_sem, w_sem, own_sem, x_sem):
+           send_sem, recv_sem, credit, in_sem, wd_sem, w_sem, own_sem, x_sem):
     T, D = x.shape
     F = gate.shape[1]
     R = T // n
@@ -58,11 +58,29 @@
     def load_x(i, k):
         return pltpu.make_async_copy(x.at[:, ds(i, W)], xt.at[k], x_sem.at[k])
 
+    def hop(d, g, j, src, dst):
+        k = lax.rem(g, 2)
+        return pltpu.make_async_remote_copy(
+            src_ref=src, dst_ref=dst, send_sem=send_sem.at[d, k, j], recv_sem=recv_sem.at[d, k, j],
+            device_id={"tp": to[d]}, device_id_type=MESH)
+
     def rs(d, s, j):
-        return pltpu.make_async_remote_copy(
-            src_ref=buf.at[d, s, j], dst_ref=buf.at[d, s + 1, j],
-            send_sem=rs_send.at[d, s, j], recv_sem=rs_recv.at[d, s, j],
-            device_id={"tp": to[d]}, device_id_type=MESH)
+        return hop(d, s, j, buf.at[d, s, j], buf.at[d, s + 1, j])
+
+    def send(d, g, j, copy):
+        def ready():
+            hop(d, g, j, buf.at[d, 0, j], buf.at[d, 0, j]).wait_send()
+            pl.semaphore_wait(credit.at[d], 1)
+
+        if isinstance(g, int):
+            if g >= 2:
+                ready()
+        else:
+            pl.when(g >= 2)(ready)
+        copy.start()
+
+    def taken(d):
+        pl.semaphore_signal(credit.at[d], inc=1, device_id={"tp": to[1 - d]}, device_id_type=MESH)
 
     def rs_block(d, s):
         return mod(me - 1 - s) if d == 0 else mod(me - 1 + s)
@@ -71,26 +89,16 @@
         return dx.at[ds(b, R), ds(d * C + j, W)]
 
     def ag_first(d, j):
-        b = rs_block(d, n - 1)
-        return pltpu.make_async_remote_copy(
-            src_ref=buf.at[d, n - 1, j], dst_ref=piece(d, b, j),
-            send_sem=ag_send.at[d, 0, j], recv_sem=ag_recv.at[d, 0, j],
-            device_id={"tp": to[d]}, device_id_type=MESH)
+        return hop(d, n - 1, j, buf.at[d, n - 1, j], piece(d, rs_block(d, n - 1), j))
 
     def ag_own(d, j):
-        return pltpu.make_async_copy(buf.at[d, n - 1, j], piece(d, rs_block(d, n - 1), j), own_sem.at[d, j])
+        return pltpu.make_async_copy(buf.at[d, n - 1, j], piece(d, rs_block(d, n - 1), j), own_sem.at[d])
 
     def ag(d, a, j, b):
-        return pltpu.make_async_remote_copy(
-            src_ref=piece(d, b, j), dst_ref=piece(d, b, j),
-            send_sem=ag_send.at[d, a, j], recv_sem=ag_recv.at[d, a, j],
-            device_id={"tp": to[d]}, device_id_type=MESH)
+        return hop(d, a + n - 1, j, piece(d, b, j), piece(d, b, j))
 
     def ag_end(d, j, b):
-        return pltpu.make_async_remote_copy(
-            src_ref=piece(d, b, j), dst_ref=(end_r, end_l)[d].at[:, ds(j, W)],
-            send_sem=ag_send.at[d, n - 3, j], recv_sem=ag_recv.at[d, n - 3, j],
-            device_id={"tp": to[d]}, device_id_type=MESH)
+        return hop(d, 2 * n - 4, j, piece(d, b, j), (end_r, end_l)[d].at[:, ds(j, W)])
 
     def ag_in(d, a):
         return mod(me - 1 - a) if d == 0 else mod(me - 1 + a)
@@ -122,25 +130,31 @@
             for d in (0, 1):
                 for c in load_w(d * C + j):
                     c.wait()
+                buf[d, s, j] = term(d, s, j).astype(BF)
+                send(d, s, j, rs(d, s, j))
         else:
             for d in (0, 1):
                 rs(d, s - 1, j).wait_recv()
+                taken(d)
         if blocks:
             @pl.when(j == 0)
             def _():
                 for b in blocks:
                     wait_block(b)
-        sums = [term(d, s, j) for d in (0, 1)]
         if not first:
-            sums = [buf[d, s, j].astype(F32) + sums[d] for d in (0, 1)]
-        for d in (0, 1):
-            buf[d, s, j] = sums[d].astype(BF)
-        for d in (0, 1):
-            if last:
-                ag_first(d, j).start()
-                ag_own(d, j).start()
-            else:
-                rs(d, s, j).start()
+            sums = [buf[d, s, j].astype(F32) + term(d, s, j) for d in (0, 1)]
+            for d in (0, 1):
+                buf[d, s, j] = sums[d].astype(BF)
+            for d in (0, 1):
+                if last:
+                    send(d, s, j, ag_first(d, j))
+
+                    @pl.when(j > 0)
+                    def _():
+                        ag_own(d, j - 1).wait()
+                    ag_own(d, j).start()
+                else:
+                    send(d, s, j, rs(d, s, j))
         for b in blocks:
             dh(b, j)
 
@@ -161,22 +175,20 @@
     barrier = pltpu.get_barrier_semaphore()
     for p in (left, right):
         pl.semaphore_signal(barrier, inc=1, device_id={"tp": p}, device_id_type=MESH)
+
+    wait_block(order[0])
+
+    for group in (range(0, 2), range(2, FT)):
+        for j in group:
+            load_wd(j).wait()
+        for j in group:
+            if j + 1 < C:
+                start_w(j + 1)
+            if j < 2:
+                start(load_block(order[j + 1]))
+        for j in group:
+            dh(order[0], j)
     pl.semaphore_wait(barrier, 2)
-
-    wait_block(order[0])
-
-    @pl.loop(0, FT)
-    def _(j):
-        load_wd(j).wait()
-
-        @pl.when(j + 1 < C)
-        def _():
-            start_w(j + 1)
-        for k in (0, 1):
-            @pl.when(j == k)
-            def _():
-                start(load_block(order[k + 1]))
-        dh(order[0], j)
 
     @pl.loop(0, C)
     def _(j):
@@ -206,11 +218,6 @@
     def _(j):
         rs_slot(n - 1, j, last=True)
 
-    @pl.loop(0, (n - 1) * C)
-    def _(q):
-        for d in (0, 1):
-            rs(d, q // C, lax.rem(q, C)).wait_send()
-
     def forward(q):
         a, j = q // C, lax.rem(q, C)
         for d in (0, 1):
@@ -220,17 +227,18 @@
             def _():
                 ag(d, a, j, b).wait_recv()
 
+            @pl.when(a == n - 3)
+            def _():
+                ag_end(d, j, b).wait_recv()
+
             @pl.when(a < n - 4)
             def _():
-                ag(d, a + 1, j, b).start()
+                taken(d)
+                send(d, a + n, j, ag(d, a + 1, j, b))
 
             @pl.when(a == n - 4)
             def _():
-                ag_end(d, j, b).start()
-
-            @pl.when(a == n - 3)
-            def _():
-                ag_end(d, j, b).wait_recv()
+                send(d, 2 * n - 4, j, ag_end(d, j, b))
 
     @pl.loop(0, D // W)
     def _(i):
@@ -253,14 +261,11 @@
     @pl.loop(0, C)
     def _(j):
         for d in (0, 1):
-            ag_own(d, j).wait()
-            ag_first(d, j).wait_send()
-            ag_end(d, j, me).wait_send()
-
-    @pl.loop(C, (n - 3) * C)
-    def _(q):
-        for d in (0, 1):
-            ag(d, q // C, lax.rem(q, C), me).wait_send()
+            for g in (2 * n - 5, 2 * n - 4):
+                hop(d, g, j, buf.at[d, 0, j], buf.at[d, 0, j]).wait_send()
+
+    for d in (0, 1):
+        ag_own(d, C - 1).wait()
 
 
 def half(ref, b, R, d):
@@ -332,8 +337,8 @@
                 pltpu.VMEM((T, F), BF),
                 pltpu.VMEM((2, n, C, R, W), BF),
                 pltpu.VMEM((2, T, W), BF),
-                dma((2, n - 1, C)), dma((2, n - 1, C)), dma((2, n - 2, C)), dma((2, n - 2, C)),
-                dma((3, n)), dma((FT,)), dma((2, 2 * C)), dma((2, C)), dma((2,)),
+                dma((2, 2, C)), dma((2, 2, C)), pltpu.SemaphoreType.REGULAR((2,)),
+                dma((3, n)), dma((FT,)), dma((2, 2 * C)), dma((2,)), dma((2,)),
             ],
             compiler_params=pltpu.CompilerParams(
                 collective_id=0, has_side_effects=True, vmem_limit_bytes=44 << 20),

time: 221 us -> 221 us (level)
  no operation moved by 1% of the time
where the time goes in v2:
time: 221 us; the launch traced here: 220 us
  Pallas kernels  214 us (97%)
  starting transfers between devices  3.32 us (2%)
    pallas_call x1, Pallas kernels, step(): pl.pallas_call(functools.partial(kernel, n), out_shape=[shape(T, D), shap...  201 us
    pallas_call x1, Pallas kernels, step(): pl.pallas_call(functools.partial(copy_kernel, n), out_shape=[shape(T, D)]...  12.4 us
  transfers between devices with their start and end apart: 2, of which 1 were waited for; matrix products, arithmetic and copies ran while one was open for 0% of the time, Pallas kernels for 6%

profile of v2, /device:TPU:22, one launch (start us, length us, event | category | flops | bytes accessed | tf_op | source)
XLA Modules:
  0.0 220.5 jit_solution(6173671299471598688)
XLA Ops:
  0.6 201.0 %mlp_bwd.1 = (bf16[2048,2560]{1,0:T(8,128)(2,1)}, bf16[256,1280]{1,0:T(8,128)(2,1)}, bf16[256,1280]{1,0:T(8,128)(2,1)}, bf16[2560,1280]{1,0:T(8,128)(2,1)S(1)}, ...) custom-call(bf16[2048,2560]{1,0:T(8,128)(2,1)} %x.1, bf16[2048,2560]{1,0:T(8,128)(2,1)} %dy.1, ...), custom_call_target="tpu_custom_call" | custom-call | tf_op jit(solution)/shard_map/mlp_bwd/pallas_call | solution.py:329
  201.6 0.1 collective-permute-start
  201.7 3.2 %collective-permute-start.1 = (bf16[256,1280]{1,0:T(8,128)(2,1)}, bf16[256,1280]{1,0:T(8,128)(2,1)S(1)}, u32[]{:S(2)}, u32[]{:S(2)}) collective-permute-start(bf16[256,1280]{1,0:T(8,128)(2,1)} %get-tuple-element.16.end_l), channel_id=1, source_target_pairs={{0,7},{1,0},{2,1},{3,2},{4,3},{5,4},{6,5},{7,6},{8,15},{9,8},{10,9... | collective-permute-start | bytes 1966088 | tf_op jit(solution)/shard_map/ppermute | solution.py:350
  204.9 12.4 %place.1 = (bf16[2048,2560]{1,0:T(8,128)(2,1)}, bf16[2560,1280]{1,0:T(8,128)(2,1)}, bf16[2560,1280]{1,0:T(8,128)(2,1)}, bf16[1280,2560]{1,0:T(8,128)(2,1)}) custom-call(bf16[2048,2560]{1,0:T(8,128)(2,1)} %get-tuple-element.14.dx, bf16[256,1280]{1,0:T(8,128)(2,1)} %get-tuple-element.15.end_r, bf16[256,1280]{1,0:T(8,128)(2,1)} %get-tuple-element.16.end_l, ...), custom_call_target="tpu_custom_call" | custom-call | flops 12999999488 | bytes 41000000 | tf_op jit(solution)/shard_map/place/pallas_call | solution.py:352
  217.4 1.9 collective-permute-done.got_r
  219.3 0.0 collective-permute-done.1.got_l
  219.3 1.1 place_end.1
Async XLA Ops:
  201.6 17.7 %collective-permute-start = (bf16[256,1280]{1,0:T(8,128)(2,1)}, bf16[256,1280]{1,0:T(8,128)(2,1)S(1)}, u32[]{:S(2)}, u32[]{:S(2)}) collective-permute-start(bf16[256,1280]{1,0:T(8,128)(2,1)} %get-tuple-element.15.end_r), channel_id=1, source_target_pairs={{0,1},{1,2},{2,3},{3,4},{4,5},{5,6},{6,7},{7,0},{8,9},{9,10},{10,1... | collective-permute-start | bytes 1966088 | tf_op jit(solution)/shard_map/ppermute | solution.py:349
  201.7 17.5 %collective-permute-start.1 = (bf16[256,1280]{1,0:T(8,128)(2,1)}, bf16[256,1280]{1,0:T(8,128)(2,1)S(1)}, u32[]{:S(2)}, u32[]{:S(2)}) collective-permute-start(bf16[256,1280]{1,0:T(8,128)(2,1)} %get-tuple-element.16.end_l), channel_id=1, source_target_pairs={{0,7},{1,0},{2,1},{3,2},{4,3},{5,4},{6,5},{7,6},{8,15},{9,8},{10,9... | collective-permute-start | bytes 1966088 | tf_op jit(solution)/shard_map/ppermute | solution.py:350

commit v3 on v2

--- a/solution.py
+++ b/solution.py
@@ -130,31 +130,35 @@
             for d in (0, 1):
                 for c in load_w(d * C + j):
                     c.wait()
-                buf[d, s, j] = term(d, s, j).astype(BF)
-                send(d, s, j, rs(d, s, j))
         else:
             for d in (0, 1):
                 rs(d, s - 1, j).wait_recv()
                 taken(d)
-        if blocks:
+        if blocks and not first:
             @pl.when(j == 0)
             def _():
                 for b in blocks:
                     wait_block(b)
+        sums = [term(d, s, j) for d in (0, 1)]
         if not first:
-            sums = [buf[d, s, j].astype(F32) + term(d, s, j) for d in (0, 1)]
-            for d in (0, 1):
-                buf[d, s, j] = sums[d].astype(BF)
-            for d in (0, 1):
-                if last:
-                    send(d, s, j, ag_first(d, j))
-
-                    @pl.when(j > 0)
-                    def _():
-                        ag_own(d, j - 1).wait()
-                    ag_own(d, j).start()
-                else:
-                    send(d, s, j, rs(d, s, j))
+            sums = [buf[d, s, j].astype(F32) + sums[d] for d in (0, 1)]
+        for d in (0, 1):
+            buf[d, s, j] = sums[d].astype(BF)
+        for d in (0, 1):
+            if last:
+                send(d, s, j, ag_first(d, j))
+
+                @pl.when(j > 0)
+                def _():
+                    ag_own(d, j - 1).wait()
+                ag_own(d, j).start()
+            else:
+                send(d, s, j, rs(d, s, j))
+        if blocks and first:
+            @pl.when(j == 0)
+            def _():
+                for b in blocks:
+                    wait_block(b)
         for b in blocks:
             dh(b, j)
 
@@ -169,23 +173,24 @@
             start(load_w(d * C + j))
 
     start(load_block(order[0]))
-    start([load_wd(j) for j in range(FT)])
-    start_w(0)
+    start([load_wd(j) for j in range(2)])
 
     barrier = pltpu.get_barrier_semaphore()
     for p in (left, right):
         pl.semaphore_signal(barrier, inc=1, device_id={"tp": p}, device_id_type=MESH)
 
     wait_block(order[0])
+    start([load_wd(j) for j in range(2, FT)])
+    start_w(0)
+    for b in order[1:3]:
+        start(load_block(b))
 
     for group in (range(0, 2), range(2, FT)):
         for j in group:
             load_wd(j).wait()
-        for j in group:
-            if j + 1 < C:
-                start_w(j + 1)
-            if j < 2:
-                start(load_block(order[j + 1]))
+        if 2 in group:
+            for j in range(1, C):
+                start_w(j)
         for j in group:
             dh(order[0], j)
     pl.semaphore_wait(barrier, 2)
@@ -239,6 +244,10 @@
             @pl.when(a == n - 4)
             def _():
                 send(d, 2 * n - 4, j, ag_end(d, j, b))
+
+    ahead = 2
+    for q in range(ahead):
+        forward(q)
 
     @pl.loop(0, D // W)
     def _(i):
@@ -246,7 +255,7 @@
         load_x(i, k).wait()
         for h, out in ((0, dwg), (1, dwu)):
             out[ds(i, W), :] = tn(xt[k], dgu[h]).astype(BF)
-            forward(2 * i + h)
+            forward(2 * i + h + ahead)
 
         @pl.when(i + 2 < D // W)
         def _():
@@ -256,7 +265,15 @@
     def _(i):
         for h in (0, 1):
             dwd[ds(i, W), h * H:(h + 1) * H] = tn(hid[:, ds(i, W)], dy_v[:, h * H:(h + 1) * H]).astype(BF)
-            forward(2 * (D // W) + 2 * i + h)
+            q = 2 * (D // W) + 2 * i + h + ahead
+
+            @pl.when(q < (n - 3) * C)
+            def _():
+                forward(q)
+
+    @pl.loop((n - 3) * C, (n - 2) * C)
+    def _(q):
+        forward(q)
 
     @pl.loop(0, C)
     def _(j):

time: 221 us -> 220 us (level)
  no operation moved by 1% of the time
where the time goes in v3:
time: 220 us
  Pallas kernels  214 us (97%)
  starting transfers between devices  3.32 us (2%)
    pallas_call x1, Pallas kernels, step(): pl.pallas_call(functools.partial(kernel, n), out_shape=[shape(T, D), shap...  201 us
    pallas_call x1, Pallas kernels, step(): pl.pallas_call(functools.partial(copy_kernel, n), out_shape=[shape(T, D)]...  12.4 us
  transfers between devices with their start and end apart: 2, of which 1 were waited for; matrix products, arithmetic and copies ran while one was open for 0% of the time, Pallas kernels for 6%

profile of v3, /device:TPU:22, one launch (start us, length us, event | category | flops | bytes accessed | tf_op | source)
XLA Modules:
  0.0 220.1 jit_solution(8395490972167582155)
XLA Ops:
  0.6 200.6 %mlp_bwd.1 = (bf16[2048,2560]{1,0:T(8,128)(2,1)}, bf16[256,1280]{1,0:T(8,128)(2,1)}, bf16[256,1280]{1,0:T(8,128)(2,1)}, bf16[2560,1280]{1,0:T(8,128)(2,1)S(1)}, ...) custom-call(bf16[2048,2560]{1,0:T(8,128)(2,1)} %x.1, bf16[2048,2560]{1,0:T(8,128)(2,1)} %dy.1, ...), custom_call_target="tpu_custom_call" | custom-call | tf_op jit(solution)/shard_map/mlp_bwd/pallas_call | solution.py:346
  201.2 0.1 collective-permute-start
  201.4 3.2 %collective-permute-start.1 = (bf16[256,1280]{1,0:T(8,128)(2,1)}, bf16[256,1280]{1,0:T(8,128)(2,1)S(1)}, u32[]{:S(2)}, u32[]{:S(2)}) collective-permute-start(bf16[256,1280]{1,0:T(8,128)(2,1)} %get-tuple-element.16.end_l), channel_id=1, source_target_pairs={{0,7},{1,0},{2,1},{3,2},{4,3},{5,4},{6,5},{7,6},{8,15},{9,8},{10,9... | collective-permute-start | bytes 1966088 | tf_op jit(solution)/shard_map/ppermute | solution.py:367
  204.6 12.4 %place.1 = (bf16[2048,2560]{1,0:T(8,128)(2,1)}, bf16[2560,1280]{1,0:T(8,128)(2,1)}, bf16[2560,1280]{1,0:T(8,128)(2,1)}, bf16[1280,2560]{1,0:T(8,128)(2,1)}) custom-call(bf16[2048,2560]{1,0:T(8,128)(2,1)} %get-tuple-element.14.dx, bf16[256,1280]{1,0:T(8,128)(2,1)} %get-tuple-element.15.end_r, bf16[256,1280]{1,0:T(8,128)(2,1)} %get-tuple-element.16.end_l, ...), custom_call_target="tpu_custom_call" | custom-call | flops 12999999488 | bytes 41000000 | tf_op jit(solution)/shard_map/place/pallas_call | solution.py:369
  217.0 1.9 collective-permute-done.got_r
  218.9 0.0 collective-permute-done.1.got_l
  218.9 1.1 place_end.1
Async XLA Ops:
  201.2 17.6 %collective-permute-start = (bf16[256,1280]{1,0:T(8,128)(2,1)}, bf16[256,1280]{1,0:T(8,128)(2,1)S(1)}, u32[]{:S(2)}, u32[]{:S(2)}) collective-permute-start(bf16[256,1280]{1,0:T(8,128)(2,1)} %get-tuple-element.15.end_r), channel_id=1, source_target_pairs={{0,1},{1,2},{2,3},{3,4},{4,5},{5,6},{6,7},{7,0},{8,9},{9,10},{10,1... | collective-permute-start | bytes 1966088 | tf_op jit(solution)/shard_map/ppermute | solution.py:366
  201.4 17.5 %collective-permute-start.1 = (bf16[256,1280]{1,0:T(8,128)(2,1)}, bf16[256,1280]{1,0:T(8,128)(2,1)S(1)}, u32[]{:S(2)}, u32[]{:S(2)}) collective-permute-start(bf16[256,1280]{1,0:T(8,128)(2,1)} %get-tuple-element.16.end_l), channel_id=1, source_target_pairs={{0,7},{1,0},{2,1},{3,2},{4,3},{5,4},{6,5},{7,6},{8,15},{9,8},{10,9... | collective-permute-start | bytes 1966088 | tf_op jit(solution)/shard_map/ppermute | solution.py:367

commit v4 on v3

--- a/solution.py
+++ b/solution.py
@@ -181,22 +181,25 @@
 
     wait_block(order[0])
     start([load_wd(j) for j in range(2, FT)])
-    start_w(0)
-    for b in order[1:3]:
-        start(load_block(b))
 
     for group in (range(0, 2), range(2, FT)):
         for j in group:
             load_wd(j).wait()
-        if 2 in group:
-            for j in range(1, C):
-                start_w(j)
+        if 0 in group:
+            start_w(0)
+        else:
+            for b in order[1:3]:
+                start(load_block(b))
         for j in group:
             dh(order[0], j)
+    start_w(1)
     pl.semaphore_wait(barrier, 2)
 
     @pl.loop(0, C)
     def _(j):
+        @pl.when(j + 2 < C)
+        def _():
+            start_w(j + 2)
         for k in range(5):
             @pl.when(j == k)
             def _():
@@ -293,18 +296,20 @@
 def copy_kernel(n, dx, end_r, end_l, dwg, dwu, dwd, dx_o, dwg_o, dwu_o, dwd_o, stage, in_sem, out_sem, w_sem):
     R = dx.shape[0] // n
     me = lax.axis_index("tp")
-    parts = []
+    parts, whole = [], []
     for d, end in ((0, end_r), (1, end_l)):
         for a in range(-1, n - 2):
             b = lax.rem((me - 1 - a if d == 0 else me - 1 + a) + 2 * n, n)
             if d == 1 and a == -1:
                 b = lax.rem(me - 2 + n, n)
-            src = end if a == n - 3 else half(dx, b, R, d)
+            if a == n - 3:
+                whole.append((end, half(dx_o, b, R, d)))
+                continue
             i = len(parts)
-            parts.append((pltpu.make_async_copy(src, stage.at[i], in_sem.at[i]),
+            parts.append((pltpu.make_async_copy(half(dx, b, R, d), stage.at[i], in_sem.at[i]),
                           pltpu.make_async_copy(stage.at[i], half(dx_o, b, R, d), out_sem.at[i])))
     whole = [pltpu.make_async_copy(v, o, w_sem.at[i])
-             for i, (v, o) in enumerate(((dwg, dwg_o), (dwu, dwu_o), (dwd, dwd_o)))]
+             for i, (v, o) in enumerate(whole + [(dwg, dwg_o), (dwu, dwu_o), (dwd, dwd_o)])]
     for load, _ in parts:
         load.start()
     for c in whole:
@@ -342,12 +347,13 @@
         vmem = pl.BlockSpec(memory_space=pltpu.VMEM)
         hbm = pl.BlockSpec(memory_space=pltpu.HBM)
         shape = lambda *s: jax.ShapeDtypeStruct(s, BF)
+        ends = [shape(R, D // 2)] * 2
         dws = [shape(D, F), shape(D, F), shape(F, D)]
         dx, end_r, end_l, *dw = pl.pallas_call(
             functools.partial(kernel, n),
-            out_shape=[shape(T, D), shape(R, D // 2), shape(R, D // 2)] + [pltpu.VMEM(w.shape, BF) for w in dws],
+            out_shape=[shape(T, D)] + [pltpu.VMEM(w.shape, BF) for w in ends + dws],
             in_specs=[any_] * 7,
-            out_specs=[any_] * 3 + [vmem] * 3,
+            out_specs=[any_] + [vmem] * 5,
             scratch_shapes=[
                 pltpu.VMEM((T, D), BF),
                 pltpu.VMEM((2, T, F), BF),
@@ -358,24 +364,24 @@
                 dma((3, n)), dma((FT,)), dma((2, 2 * C)), dma((2,)), dma((2,)),
             ],
             compiler_params=pltpu.CompilerParams(
-                collective_id=0, has_side_effects=True, vmem_limit_bytes=44 << 20),
+                collective_id=0, has_side_effects=True, vmem_limit_bytes=43 << 20),
             name="mlp_bwd",
         )(x, dy, gate, up, w_gate, w_up, w_down)
         ahead = [(i, (i + 1) % n) for i in range(n)]
         back = [(i, (i - 1) % n) for i in range(n)]
         got_r = lax.ppermute(end_r, "tp", ahead)
         got_l = lax.ppermute(end_l, "tp", back)
-        m = 2 * (n - 1)
+        m = 2 * (n - 2)
         dx, *dw = pl.pallas_call(
             functools.partial(copy_kernel, n),
             out_shape=[shape(T, D)] + dws,
-            in_specs=[hbm] * 3 + [vmem] * 3,
+            in_specs=[hbm] + [vmem] * 5,
             out_specs=[hbm] * 4,
-            scratch_shapes=[pltpu.VMEM((m, R, D // 2), BF), dma((m,)), dma((m,)), dma((3,))],
+            scratch_shapes=[pltpu.VMEM((m, R, D // 2), BF), dma((m,)), dma((m,)), dma((5,))],
             compiler_params=pltpu.CompilerParams(vmem_limit_bytes=10 << 20),
             cost_estimate=pl.CostEstimate(flops=13_000_000_000, bytes_accessed=41_000_000, transcendentals=0),
             name="place",
-        )(*(pltpu.with_memory_space_constraint(v, pltpu.HBM) for v in (dx, end_r, end_l)), *dw)
+        )(pltpu.with_memory_space_constraint(dx, pltpu.HBM), end_r, end_l, *dw)
         dx = pl.pallas_call(
             functools.partial(end_kernel, n),
             out_shape=shape(T, D),

time: 220 us -> 218 us (level)
  transfers between devices with their start and end apart: 2 -> 2, of which waited for: 1 -> 1; matrix products, arithmetic and copies ran while one was open for 0% -> 0% of each run, Pallas kernels for 6% -> 5%
where the time goes in v4:
time: 218 us
  Pallas kernels  212 us (97%)
  starting transfers between devices  3.32 us (2%)
  waiting for transfers between devices  2.21 us (1%)
    pallas_call x1, Pallas kernels, step(): pl.pallas_call(functools.partial(kernel, n), out_shape=[shape(T, D)] + [p...  199 us
    pallas_call x1, Pallas kernels, step(): pl.pallas_call(functools.partial(copy_kernel, n), out_shape=[shape(T, D)]...  12 us
  transfers between devices with their start and end apart: 2, of which 1 were waited for; matrix products, arithmetic and copies ran while one was open for 0% of the time, Pallas kernels for 5%

profile of v4, /device:TPU:22, one launch (start us, length us, event | category | flops | bytes accessed | tf_op | source)
XLA Modules:
  0.0 218.1 jit_solution(5666770797255847025)
XLA Ops:
  0.6 198.7 %mlp_bwd.1 = (bf16[2048,2560]{1,0:T(8,128)(2,1)}, bf16[256,1280]{1,0:T(8,128)(2,1)S(1)}, bf16[256,1280]{1,0:T(8,128)(2,1)S(1)}, bf16[2560,1280]{1,0:T(8,128)(2,1...) custom-call(bf16[2048,2560]{1,0:T(8,128)(2,1)} %x.1, bf16[2048,2560]{1,0:T(8,128)(2,1)} %dy.1, ...), custom_call_target="tpu_custom_call" | custom-call | tf_op jit(solution)/shard_map/mlp_bwd/pallas_call | solution.py:352
  199.4 0.1 collective-permute-start
  199.5 3.2 %collective-permute-start.1 = (bf16[256,1280]{1,0:T(8,128)(2,1)S(1)}, bf16[256,1280]{1,0:T(8,128)(2,1)S(1)}, u32[]{:S(2)}, u32[]{:S(2)}) collective-permute-start(bf16[256,1280]{1,0:T(8,128)(2,1)S(1)} %get-tuple-element.16.end_l), channel_id=1, source_target_pairs={{0,7},{1,0},{2,1},{3,2},{4,3},{5,4},{6,5},{7,6},{8,15},{9,8},{10,9... | collective-permute-start | bytes 1966088 | tf_op jit(solution)/shard_map/ppermute | solution.py:373
  202.7 12.0 %place.1 = (bf16[2048,2560]{1,0:T(8,128)(2,1)}, bf16[2560,1280]{1,0:T(8,128)(2,1)}, bf16[2560,1280]{1,0:T(8,128)(2,1)}, bf16[1280,2560]{1,0:T(8,128)(2,1)}) custom-call(bf16[2048,2560]{1,0:T(8,128)(2,1)} %get-tuple-element.14.dx, bf16[256,1280]{1,0:T(8,128)(2,1)S(1)} %get-tuple-element.15.end_r, bf16[256,1280]{1,0:T(8,128)(2,1)S(1)} %get-tuple-element.16.end_l, ...), custom_call_target="tpu_custom_call" | custom-call | flops 12999999488 | bytes 41000000 | tf_op jit(solution)/shard_map/place/pallas_call | solution.py:375
  214.7 2.2 %collective-permute-done.got_r = bf16[256,1280]{1,0:T(8,128)(2,1)S(1)} collective-permute-done((bf16[256,1280]{1,0:T(8,128)(2,1)S(1)}, bf16[256,1280]{1,0:T(8,128)(2,1)S(1)}, u32[]{:S(2)}, u32[]{:S(2)}) %collective-permute-start) | collective-permute-done | bytes 655392 | tf_op jit(solution)/shard_map/ppermute | solution.py:372
  216.9 0.0 collective-permute-done.1.got_l
  216.9 1.1 place_end.1
Async XLA Ops:
  199.4 17.5 %collective-permute-start = (bf16[256,1280]{1,0:T(8,128)(2,1)S(1)}, bf16[256,1280]{1,0:T(8,128)(2,1)S(1)}, u32[]{:S(2)}, u32[]{:S(2)}) collective-permute-start(bf16[256,1280]{1,0:T(8,128)(2,1)S(1)} %get-tuple-element.15.end_r), channel_id=1, source_target_pairs={{0,1},{1,2},{2,3},{3,4},{4,5},{5,6},{6,7},{7,0},{8,9},{9,10},{10,1... | collective-permute-start | bytes 1966088 | tf_op jit(solution)/shard_map/ppermute | solution.py:372
  199.5 17.4 %collective-permute-start.1 = (bf16[256,1280]{1,0:T(8,128)(2,1)S(1)}, bf16[256,1280]{1,0:T(8,128)(2,1)S(1)}, u32[]{:S(2)}, u32[]{:S(2)}) collective-permute-start(bf16[256,1280]{1,0:T(8,128)(2,1)S(1)} %get-tuple-element.16.end_l), channel_id=1, source_target_pairs={{0,7},{1,0},{2,1},{3,2},{4,3},{5,4},{6,5},{7,6},{8,15},{9,8},{10,9... | collective-permute-start | bytes 1966088 | tf_op jit(solution)/shard_map/ppermute | solution.py:373

commit v5 on v4

--- a/solution.py
+++ b/solution.py
@@ -42,18 +42,19 @@
     def ds(i, size):
         return pl.ds(pl.multiple_of(i * size, size), size)
 
-    def load_block(b):
-        rows = ds(b, R)
-        return (pltpu.make_async_copy(dy.at[rows, :], dy_v.at[rows, :], in_sem.at[0, b]),
-                pltpu.make_async_copy(gate.at[rows, :], dgu.at[0, rows, :], in_sem.at[1, b]),
-                pltpu.make_async_copy(up.at[rows, :], dgu.at[1, rows, :], in_sem.at[2, b]))
+    def load_block(b, i):
+        rows, k = ds(b, R), lax.rem(i, 6)
+        return (pltpu.make_async_copy(dy.at[rows, :], dy_v.at[rows, :], in_sem.at[0, k]),
+                pltpu.make_async_copy(gate.at[rows, :], dgu.at[0, rows, :], in_sem.at[1, k]),
+                pltpu.make_async_copy(up.at[rows, :], dgu.at[1, rows, :], in_sem.at[2, k]))
 
     def load_wd(j):
         return pltpu.make_async_copy(wd.at[ds(j, W), :], dwd.at[ds(j, W), :], wd_sem.at[j])
 
-    def load_w(t):
-        return (pltpu.make_async_copy(wg.at[ds(t, W), :], dwg.at[ds(t, W), :], w_sem.at[0, t]),
-                pltpu.make_async_copy(wu.at[ds(t, W), :], dwu.at[ds(t, W), :], w_sem.at[1, t]))
+    def load_w(d, j):
+        t, k = d * C + j, lax.rem(j, 3)
+        return (pltpu.make_async_copy(wg.at[ds(t, W), :], dwg.at[ds(t, W), :], w_sem.at[0, d, k]),
+                pltpu.make_async_copy(wu.at[ds(t, W), :], dwu.at[ds(t, W), :], w_sem.at[1, d, k]))
 
     def load_x(i, k):
         return pltpu.make_async_copy(x.at[:, ds(i, W)], xt.at[k], x_sem.at[k])
@@ -103,8 +104,8 @@
     def ag_in(d, a):
         return mod(me - 1 - a) if d == 0 else mod(me - 1 + a)
 
-    def wait_block(b):
-        for c in load_block(b):
+    def wait_block(b, i):
+        for c in load_block(b, i):
             c.wait()
 
     def dh(b, j):
@@ -113,10 +114,10 @@
         g = dgu[0, rows, cols].astype(F32)
         u = dgu[1, rows, cols].astype(F32)
         g2 = g * g
-        t = jnp.tanh(ROOT * (g + CUBE * (g2 * g)))
-        cdf = 0.5 * (1.0 + t)
+        t = jnp.tanh(g * (ROOT + (ROOT * CUBE) * g2))
+        cdf = 0.5 + 0.5 * t
         act = g * cdf
-        slope = cdf + g * (0.5 * (1.0 - t * t)) * (ROOT * (1.0 + (3.0 * CUBE) * g2))
+        slope = cdf + (act * (1.0 - t)) * (ROOT + (3.0 * ROOT * CUBE) * g2)
         hid[rows, cols] = (act * u).astype(BF)
         dgu[0, rows, cols] = (d * u * slope).astype(BF)
         dgu[1, rows, cols] = (d * act).astype(BF)
@@ -128,7 +129,7 @@
     def rs_slot(s, j, first=False, last=False, blocks=()):
         if first:
             for d in (0, 1):
-                for c in load_w(d * C + j):
+                for c in load_w(d, j):
                     c.wait()
         else:
             for d in (0, 1):
@@ -137,8 +138,8 @@
         if blocks and not first:
             @pl.when(j == 0)
             def _():
-                for b in blocks:
-                    wait_block(b)
+                for i, b in enumerate(blocks):
+                    wait_block(b, 2 * s + 1 + i)
         sums = [term(d, s, j) for d in (0, 1)]
         if not first:
             sums = [buf[d, s, j].astype(F32) + sums[d] for d in (0, 1)]
@@ -157,8 +158,8 @@
         if blocks and first:
             @pl.when(j == 0)
             def _():
-                for b in blocks:
-                    wait_block(b)
+                for i, b in enumerate(blocks):
+                    wait_block(b, 2 * s + 1 + i)
         for b in blocks:
             dh(b, j)
 
@@ -170,26 +171,26 @@
 
     def start_w(j):
         for d in (0, 1):
-            start(load_w(d * C + j))
-
-    start(load_block(order[0]))
-    start([load_wd(j) for j in range(2)])
+            start(load_w(d, j))
+
+    start(load_block(order[0], 0))
+    start([load_wd(j) for j in range(3)])
 
     barrier = pltpu.get_barrier_semaphore()
     for p in (left, right):
         pl.semaphore_signal(barrier, inc=1, device_id={"tp": p}, device_id_type=MESH)
 
-    wait_block(order[0])
-    start([load_wd(j) for j in range(2, FT)])
-
-    for group in (range(0, 2), range(2, FT)):
+    wait_block(order[0], 0)
+    start([load_wd(j) for j in range(3, FT)])
+
+    for group in (range(0, 3), range(3, FT)):
         for j in group:
             load_wd(j).wait()
         if 0 in group:
             start_w(0)
         else:
-            for b in order[1:3]:
-                start(load_block(b))
+            for i in (1, 2):
+                start(load_block(order[i], i))
         for j in group:
             dh(order[0], j)
     start_w(1)
@@ -203,7 +204,7 @@
         for k in range(5):
             @pl.when(j == k)
             def _():
-                start(load_block(order[k + 3]))
+                start(load_block(order[k + 3], k + 3))
         rs_slot(0, j, first=True, blocks=(mod(me - 2), me))
 
     @pl.loop(0, 2 * C)
@@ -326,8 +327,11 @@
 def end_kernel(n, dx, got_r, got_l, dx_o, sem):
     R = dx.shape[0] // n
     me = lax.axis_index("tp")
-    copies = [pltpu.make_async_copy(got_r, half(dx_o, lax.rem(me + 1, n), R, 0), sem.at[0]),
-              pltpu.make_async_copy(got_l, half(dx_o, lax.rem(me + n - 3, n), R, 1), sem.at[1])]
+    copies = []
+    for d, got, b in ((0, got_r, lax.rem(me + 1, n)), (1, got_l, lax.rem(me + n - 3, n))):
+        for i in range(4):
+            rows = pl.ds(i * R // 4, R // 4)
+            copies.append(pltpu.make_async_copy(got.at[rows, :], half(dx_o, b, R, d).at[rows, :], sem.at[d, i]))
     for c in copies:
         c.start()
     for c in copies:
@@ -361,7 +365,7 @@
                 pltpu.VMEM((2, n, C, R, W), BF),
                 pltpu.VMEM((2, T, W), BF),
                 dma((2, 2, C)), dma((2, 2, C)), pltpu.SemaphoreType.REGULAR((2,)),
-                dma((3, n)), dma((FT,)), dma((2, 2 * C)), dma((2,)), dma((2,)),
+                dma((3, 6)), dma((FT,)), dma((2, 2, 3)), dma((2,)), dma((2,)),
             ],
             compiler_params=pltpu.CompilerParams(
                 collective_id=0, has_side_effects=True, vmem_limit_bytes=43 << 20),
@@ -387,7 +391,7 @@
             out_shape=shape(T, D),
             in_specs=[any_, vmem, vmem],
             out_specs=any_,
-            scratch_shapes=[dma((2,))],
+            scratch_shapes=[dma((2, 4))],
             input_output_aliases={0: 0},
             compiler_params=pltpu.CompilerParams(vmem_limit_bytes=1 << 20),
             name="place_end",

time: 218 us -> 217 us (level)
  transfers between devices with their start and end apart: 2 -> 2, of which waited for: 1 -> 1; matrix products, arithmetic and copies ran while one was open for 0% -> 0% of each run, Pallas kernels for 5% -> 6%
where the time goes in v5:
time: 217 us
  Pallas kernels  211 us (97%)
  starting transfers between devices  3.32 us (2%)
  waiting for transfers between devices  2.2 us (1%)
    pallas_call x1, Pallas kernels, step(): pl.pallas_call(functools.partial(kernel, n), out_shape=[shape(T, D)] + [p...  198 us
    pallas_call x1, Pallas kernels, step(): pl.pallas_call(functools.partial(copy_kernel, n), out_shape=[shape(T, D)]...  12 us
  transfers between devices with their start and end apart: 2, of which 1 were waited for; matrix products, arithmetic and copies ran while one was open for 0% of the time, Pallas kernels for 6%

profile of v5, /device:TPU:22, one launch (start us, length us, event | category | flops | bytes accessed | tf_op | source)
XLA Modules:
  0.0 217.4 jit_solution(17058045156676515796)
XLA Ops:
  0.6 198.0 %mlp_bwd.1 = (bf16[2048,2560]{1,0:T(8,128)(2,1)}, bf16[256,1280]{1,0:T(8,128)(2,1)S(1)}, bf16[256,1280]{1,0:T(8,128)(2,1)S(1)}, bf16[2560,1280]{1,0:T(8,128)(2,1...) custom-call(bf16[2048,2560]{1,0:T(8,128)(2,1)} %x.1, bf16[2048,2560]{1,0:T(8,128)(2,1)} %dy.1, ...), custom_call_target="tpu_custom_call" | custom-call | tf_op jit(solution)/shard_map/mlp_bwd/pallas_call | solution.py:356
  198.6 0.1 collective-permute-start
  198.7 3.2 %collective-permute-start.1 = (bf16[256,1280]{1,0:T(8,128)(2,1)S(1)}, bf16[256,1280]{1,0:T(8,128)(2,1)S(1)}, u32[]{:S(2)}, u32[]{:S(2)}) collective-permute-start(bf16[256,1280]{1,0:T(8,128)(2,1)S(1)} %get-tuple-element.16.end_l), channel_id=1, source_target_pairs={{0,7},{1,0},{2,1},{3,2},{4,3},{5,4},{6,5},{7,6},{8,15},{9,8},{10,9... | collective-permute-start | bytes 1966088 | tf_op jit(solution)/shard_map/ppermute | solution.py:377
  201.9 12.0 %place.1 = (bf16[2048,2560]{1,0:T(8,128)(2,1)}, bf16[2560,1280]{1,0:T(8,128)(2,1)}, bf16[2560,1280]{1,0:T(8,128)(2,1)}, bf16[1280,2560]{1,0:T(8,128)(2,1)}) custom-call(bf16[2048,2560]{1,0:T(8,128)(2,1)} %get-tuple-element.14.dx, bf16[256,1280]{1,0:T(8,128)(2,1)S(1)} %get-tuple-element.15.end_r, bf16[256,1280]{1,0:T(8,128)(2,1)S(1)} %get-tuple-element.16.end_l, ...), custom_call_target="tpu_custom_call" | custom-call | flops 12999999488 | bytes 41000000 | tf_op jit(solution)/shard_map/place/pallas_call | solution.py:379
  213.9 2.2 %collective-permute-done.got_r = bf16[256,1280]{1,0:T(8,128)(2,1)S(1)} collective-permute-done((bf16[256,1280]{1,0:T(8,128)(2,1)S(1)}, bf16[256,1280]{1,0:T(8,128)(2,1)S(1)}, u32[]{:S(2)}, u32[]{:S(2)}) %collective-permute-start) | collective-permute-done | bytes 655392 | tf_op jit(solution)/shard_map/ppermute | solution.py:376
  216.1 0.0 collective-permute-done.1.got_l
  216.1 1.1 place_end.1
Async XLA Ops:
  198.6 17.5 %collective-permute-start = (bf16[256,1280]{1,0:T(8,128)(2,1)S(1)}, bf16[256,1280]{1,0:T(8,128)(2,1)S(1)}, u32[]{:S(2)}, u32[]{:S(2)}) collective-permute-start(bf16[256,1280]{1,0:T(8,128)(2,1)S(1)} %get-tuple-element.15.end_r), channel_id=1, source_target_pairs={{0,1},{1,2},{2,3},{3,4},{4,5},{5,6},{6,7},{7,0},{8,9},{9,10},{10,1... | collective-permute-start | bytes 1966088 | tf_op jit(solution)/shard_map/ppermute | solution.py:376
  198.7 17.4 %collective-permute-start.1 = (bf16[256,1280]{1,0:T(8,128)(2,1)S(1)}, bf16[256,1280]{1,0:T(8,128)(2,1)S(1)}, u32[]{:S(2)}, u32[]{:S(2)}) collective-permute-start(bf16[256,1280]{1,0:T(8,128)(2,1)S(1)} %get-tuple-element.16.end_l), channel_id=1, source_target_pairs={{0,7},{1,0},{2,1},{3,2},{4,3},{5,4},{6,5},{7,6},{8,15},{9,8},{10,9... | collective-permute-start | bytes 1966088 | tf_op jit(solution)/shard_map/ppermute | solution.py:377

commit v6 on v5

--- a/solution.py
+++ b/solution.py
@@ -329,8 +329,8 @@
     me = lax.axis_index("tp")
     copies = []
     for d, got, b in ((0, got_r, lax.rem(me + 1, n)), (1, got_l, lax.rem(me + n - 3, n))):
-        for i in range(4):
-            rows = pl.ds(i * R // 4, R // 4)
+        for i in range(1):
+            rows = pl.ds(i * R, R)
             copies.append(pltpu.make_async_copy(got.at[rows, :], half(dx_o, b, R, d).at[rows, :], sem.at[d, i]))
     for c in copies:
         c.start()
@@ -391,7 +391,7 @@
             out_shape=shape(T, D),
             in_specs=[any_, vmem, vmem],
             out_specs=any_,
-            scratch_shapes=[dma((2, 4))],
+            scratch_shapes=[dma((2, 1))],
             input_output_aliases={0: 0},
             compiler_params=pltpu.CompilerParams(vmem_limit_bytes=1 << 20),
             name="place_end",

time: 217 us -> 217 us (level)
  no operation moved by 1% of the time
where the time goes in v6:
time: 217 us
  Pallas kernels  211 us (97%)
  starting transfers between devices  3.32 us (2%)
  waiting for transfers between devices  2.2 us (1%)
    pallas_call x1, Pallas kernels, step(): pl.pallas_call(functools.partial(kernel, n), out_shape=[shape(T, D)] + [p...  198 us
    pallas_call x1, Pallas kernels, step(): pl.pallas_call(functools.partial(copy_kernel, n), out_shape=[shape(T, D)]...  12 us
  transfers between devices with their start and end apart: 2, of which 1 were waited for; matrix products, arithmetic and copies ran while one was open for 0% of the time, Pallas kernels for 6%

profile of v6, /device:TPU:22, one launch (start us, length us, event | category | flops | bytes accessed | tf_op | source)
XLA Modules:
  0.0 217.4 jit_solution(12558737508886596030)
XLA Ops:
  0.6 198.0 %mlp_bwd.1 = (bf16[2048,2560]{1,0:T(8,128)(2,1)}, bf16[256,1280]{1,0:T(8,128)(2,1)S(1)}, bf16[256,1280]{1,0:T(8,128)(2,1)S(1)}, bf16[2560,1280]{1,0:T(8,128)(2,1...) custom-call(bf16[2048,2560]{1,0:T(8,128)(2,1)} %x.1, bf16[2048,2560]{1,0:T(8,128)(2,1)} %dy.1, ...), custom_call_target="tpu_custom_call" | custom-call | tf_op jit(solution)/shard_map/mlp_bwd/pallas_call | solution.py:356
  198.6 0.1 collective-permute-start
  198.7 3.2 %collective-permute-start.1 = (bf16[256,1280]{1,0:T(8,128)(2,1)S(1)}, bf16[256,1280]{1,0:T(8,128)(2,1)S(1)}, u32[]{:S(2)}, u32[]{:S(2)}) collective-permute-start(bf16[256,1280]{1,0:T(8,128)(2,1)S(1)} %get-tuple-element.16.end_l), channel_id=1, source_target_pairs={{0,7},{1,0},{2,1},{3,2},{4,3},{5,4},{6,5},{7,6},{8,15},{9,8},{10,9... | collective-permute-start | bytes 1966088 | tf_op jit(solution)/shard_map/ppermute | solution.py:377
  201.9 12.0 %place.1 = (bf16[2048,2560]{1,0:T(8,128)(2,1)}, bf16[2560,1280]{1,0:T(8,128)(2,1)}, bf16[2560,1280]{1,0:T(8,128)(2,1)}, bf16[1280,2560]{1,0:T(8,128)(2,1)}) custom-call(bf16[2048,2560]{1,0:T(8,128)(2,1)} %get-tuple-element.14.dx, bf16[256,1280]{1,0:T(8,128)(2,1)S(1)} %get-tuple-element.15.end_r, bf16[256,1280]{1,0:T(8,128)(2,1)S(1)} %get-tuple-element.16.end_l, ...), custom_call_target="tpu_custom_call" | custom-call | flops 12999999488 | bytes 41000000 | tf_op jit(solution)/shard_map/place/pallas_call | solution.py:379
  213.9 2.2 %collective-permute-done.got_r = bf16[256,1280]{1,0:T(8,128)(2,1)S(1)} collective-permute-done((bf16[256,1280]{1,0:T(8,128)(2,1)S(1)}, bf16[256,1280]{1,0:T(8,128)(2,1)S(1)}, u32[]{:S(2)}, u32[]{:S(2)}) %collective-permute-start) | collective-permute-done | bytes 655392 | tf_op jit(solution)/shard_map/ppermute | solution.py:376
  216.1 0.0 collective-permute-done.1.got_l
  216.1 1.1 place_end.1
Async XLA Ops:
  198.6 17.5 %collective-permute-start = (bf16[256,1280]{1,0:T(8,128)(2,1)S(1)}, bf16[256,1280]{1,0:T(8,128)(2,1)S(1)}, u32[]{:S(2)}, u32[]{:S(2)}) collective-permute-start(bf16[256,1280]{1,0:T(8,128)(2,1)S(1)} %get-tuple-element.15.end_r), channel_id=1, source_target_pairs={{0,1},{1,2},{2,3},{3,4},{4,5},{5,6},{6,7},{7,0},{8,9},{9,10},{10,1... | collective-permute-start | bytes 1966088 | tf_op jit(solution)/shard_map/ppermute | solution.py:376
  198.7 17.4 %collective-permute-start.1 = (bf16[256,1280]{1,0:T(8,128)(2,1)S(1)}, bf16[256,1280]{1,0:T(8,128)(2,1)S(1)}, u32[]{:S(2)}, u32[]{:S(2)}) collective-permute-start(bf16[256,1280]{1,0:T(8,128)(2,1)S(1)} %get-tuple-element.16.end_l), channel_id=1, source_target_pairs={{0,7},{1,0},{2,1},{3,2},{4,3},{5,4},{6,5},{7,6},{8,15},{9,8},{10,9... | collective-permute-start | bytes 1966088 | tf_op jit(solution)/shard_map/ppermute | solution.py:377
